TPU v7x, 256 devices: a whole 4x4x8 slice. The times are simulated.
256 devices in a mesh: tm: 32 (over z, y), mp: 4 (over x), dec: 2 (over core).
Axes of the slice: x: 4, y: 4, z: 8, core: 2. Of those that a mesh axis runs over, the one named last changes fastest.
Arguments:
- latents: bfloat16 [8192, 3072], P('tm'), may hold values from -6 to 6
- modulation: float32 [32, 3, 3072], P('tm'), may hold values from -1.5 to 3.5
- w_qkv: bfloat16 [3, 3072, 3072], P(None, None, ('mp', 'dec'))
- w_out: bfloat16 [3072, 3072], P(('mp', 'dec')), may hold values from -0.109375 to 0.109375
- block_mask: int32 [32, 32], replicated, may hold values from 0 to 1, as said below
- lengths: int32 [32], replicated, may hold values from 64 to 256, as said below
Outputs:
- updated: bfloat16 [8192, 3072], P('tm', ('mp', 'dec'))
Inputs may be any that keep to these rules, and one draw needn't show every extreme that they name: block_mask[i, i] = 1 and block_mask[i, j] = 0 for j > i. `lengths`: some group of index 16 or more has all 256 tokens live.
All inputs are finite; a program needn't handle non-finite values.
Results may differ from a plain program's by a relative error of at most 0.0057.
Values may be sent and summed in bfloat16 or wider, within the bound.
A program may use at most 192 MiB of HBM per device.

v0:
```python
import jax
import jax.numpy as jnp
from jax import lax
from jax.sharding import PartitionSpec as P

HS = 128


def side_by_side(arrays, axis, dim, along):
    widths = [a.shape[along] for a in arrays]
    both = jnp.concatenate(arrays, axis=along)
    result = lax.all_gather(both, axis, axis=dim, tiled=True)
    return tuple(jnp.split(result, [sum(widths[:k]) for k in range(1, len(widths))], axis=along))


def split_up(value, dim, count):
    before, after = (value.shape[:dim], value.shape[dim + 1 :])
    return jnp.moveaxis(value.reshape(*before, count, -1, *after), dim, 0)


def sent_and_summed(value, axis, dim):
    tiles = split_up(value, dim, lax.axis_size(axis))
    arrived = lax.all_to_all(tiles, axis, split_axis=0, concat_axis=0, tiled=True)
    return arrived.astype(jnp.float32).sum(axis=0)


def shards(latents, modulation, w_qkv, w_out, block_mask, lengths):
    tok = latents.shape[0]
    columns = w_qkv.shape[2]
    heads_here = columns // HS
    groups = lengths.shape[0]
    wide = latents.astype(jnp.float32)
    mean = jnp.mean(wide, axis=-1, keepdims=True)
    var = jnp.mean((wide - mean) ** 2, axis=-1, keepdims=True)
    normed = (wide - mean) * lax.rsqrt(var + 1e-06)
    shift_row = modulation[0, 0]
    scale_row = modulation[0, 1]
    gate_row = modulation[0, 2]
    adapted = (normed * (1.0 + scale_row) + shift_row).astype(jnp.bfloat16)
    query = jnp.dot(adapted, w_qkv[0], preferred_element_type=jnp.float32).astype(jnp.bfloat16)
    key = jnp.dot(adapted, w_qkv[1], preferred_element_type=jnp.float32).astype(jnp.bfloat16)
    value = jnp.dot(adapted, w_qkv[2], preferred_element_type=jnp.float32).astype(jnp.bfloat16)
    mine = lax.axis_index("tm")
    mask_row = lax.dynamic_slice_in_dim(block_mask, mine, 1, 0)
    inv_root = 1.0 / jnp.sqrt(jnp.float32(HS))
    group_ids = jnp.arange(groups, dtype=jnp.int32)
    query_heads = query.reshape(tok, heads_here, HS)
    own_mask = jnp.broadcast_to(mask_row, (tok, groups))
    pieces = side_by_side((key, value), "tm", 0, 1)
    key_rows = pieces[0]
    value_rows = pieces[1]
    count = key_rows.shape[0]
    slots = jnp.arange(count, dtype=jnp.int32)
    key_group = slots // tok
    onehot = key_group[:, None] == group_ids[None, :]
    live_len = jnp.sum(onehot.astype(jnp.int32) * lengths[None, :], axis=1)
    wanted = jnp.dot(own_mask.astype(jnp.float32), jnp.transpose(onehot.astype(jnp.float32))) > 0.5
    allowed = wanted & (slots % tok < live_len)[None, :]

    def update(state):
        peak, total, accum = state
        key_heads = key_rows.reshape(count, heads_here, HS)
        value_heads = value_rows.reshape(count, heads_here, HS)
        score = (
            jnp.einsum("thd,shd->hts", query_heads, key_heads, preferred_element_type=jnp.float32)
            * inv_root
        )
        score = jnp.where(allowed[None, :, :], score, jnp.float32(-1e30))
        fresh = jnp.maximum(peak, jnp.max(score, axis=-1))
        weight = jnp.exp(score - fresh[:, :, None]) * allowed[None, :, :].astype(jnp.float32)
        total = jnp.sum(weight, axis=-1)
        mixed = jnp.einsum(
            "hts,shd->thd",
            weight.astype(jnp.bfloat16),
            value_heads,
            preferred_element_type=jnp.float32,
        )
        accum = mixed
        return (fresh, total, accum)

    state = lax.cond(
        jnp.any(allowed),
        update,
        lambda state: state,
        (
            jnp.full((heads_here, tok), -1e30, jnp.float32),
            jnp.zeros((heads_here, tok), jnp.float32),
            jnp.zeros((tok, heads_here, HS), jnp.float32),
        ),
    )
    peak, total, accum = state
    attended = (accum / jnp.transpose(total)[:, :, None]).reshape(tok, columns).astype(jnp.bfloat16)
    terms = jnp.dot(attended, w_out, preferred_element_type=jnp.float32)
    summed = sent_and_summed(terms.astype(jnp.bfloat16), ("mp", "dec"), 1)
    share = summed.shape[1]
    offset = lax.axis_index(("mp", "dec")) * share
    wide_here = lax.dynamic_slice_in_dim(wide, offset, share, 1)
    gate_here = lax.dynamic_slice_in_dim(gate_row, offset, share, 0)
    return (wide_here + gate_here[None, :] * summed).astype(jnp.bfloat16)


def solution(mesh):
    return jax.shard_map(
        shards,
        mesh=mesh,
        in_specs=(
            P("tm", None),
            P("tm", None, None),
            P(None, None, ("mp", "dec")),
            P(("mp", "dec"), None),
            P(),
            P(),
        ),
        out_specs=P("tm", ("mp", "dec")),
        check_vma=False,
    )
```

profile of v0, /device:TPU:1, one launch (start us, length us, event | category | flops | bytes accessed | tf_op | source)
XLA Modules:
  0.0 254.2 jit_solution(5130459519949724890)
XLA Ops:
  6.5 0.0 copy-start
  6.5 0.0 copy-start.3
  6.5 0.0 all-gather.2.cloned.1.call-start
  6.5 0.0 copy-start.2
  6.5 1.8 convert_reduce_fusion.1
  8.4 2.0 multiply_reduce_fusion
  10.4 0.0 copy-done.3
  10.4 0.0 copy-done.2
  10.4 2.7 %fusion.24 = bf16[256,384]{1,0:T(8,128)(2,1)S(1)} fusion(bf16[3,3072,384]{2,1,0:T(8,128)(2,1)} %param.10, bf16[256,3072]{1,0:T(8,128)(2,1)S(1)} %copy-done.2, f32[3072]{0:T(1024)S(1)} %bitcast.45, f32[3072]{0:T(1024)S(1)} %bitcast.48, f32[256]{0:T(256)S(1)} %add_rsqrt_fusion, f32[256]{0:T(256)S(1)} %broadcast_multiply_fusion), kind=kOutput, calls=%fused_computation.29 | convolution fusion | flops 608796672 | bytes 4155392 | tf_op jit(solution)/shard_map/dot_general | solution.py:41
  13.2 0.0 copy-start.4
  13.2 2.8 %fusion.27 = bf16[256,384]{1,0:T(8,128)(2,1)S(1)} fusion(bf16[3,3072,384]{2,1,0:T(8,128)(2,1)} %param.10, bf16[256,3072]{1,0:T(8,128)(2,1)S(1)} %copy-done.2, f32[3072]{0:T(1024)S(1)} %bitcast.46, f32[3072]{0:T(1024)S(1)} %bitcast.49, f32[256]{0:T(256)S(1)} %add_rsqrt_fusion, f32[256]{0:T(256)S(1)} %broadcast_multiply_fusion), kind=kOutput, calls=%fused_computation.30 | convolution fusion | flops 608796672 | bytes 4155392 | tf_op jit(solution)/shard_map/dot_general | solution.py:42
  15.9 0.8 pad_maximum_fusion
  16.7 0.0 all-gather.2.cloned.1.call-update
  16.8 0.7 fusion.41
  17.5 0.0 copy-done.4
  17.5 0.2 select_reduce_fusion
  17.8 4.2 %fusion.44 = (pred[]{:T(512)}, pred[256,8192]{1,0:T(8,128)(4,1)}) fusion(pred[8192]{0:T(1024)(128)(4,1)S(1)} %fusion.38, s32[8192]{0:T(1024)S(1)} %add_select_fusion, bf16[32]{0:T(256)(128)(2,1)S(1)} %fusion.41), kind=kOutput, calls=%fused_computation.59 | convolution fusion | flops 140771328 | bytes 2138177 | tf_op jit(solution)/shard_map/dot_general | solution.py:57
  22.7 3.2 %fusion.21 = bf16[256,384]{1,0:T(8,128)(2,1)S(1)} fusion(bf16[3,3072,384]{2,1,0:T(8,128)(2,1)} %param.10, bf16[256,3072]{1,0:T(8,128)(2,1)} %param.8, f32[3072]{0:T(1024)S(1)} %bitcast.47, f32[3072]{0:T(1024)S(1)} %bitcast.50, f32[256]{0:T(256)S(1)} %add_rsqrt_fusion, f32[256]{0:T(256)S(1)} %broadcast_multiply_fusion), kind=kOutput, calls=%fused_computation.28 | convolution fusion | flops 608796672 | bytes 4155392 | tf_op jit(solution)/shard_map/dot_general | solution.py:40
  25.8 113.0 %all-gather.2.cloned.1.call-done = bf16[8192,768]{1,0:T(8,128)(2,1)} async-done(((bf16[256,768]{1,0:T(8,128)(2,1)}), bf16[8192,768]{1,0:T(8,128)(2,1)}) %all-gather.2.cloned.1.call-update) | async-done | bytes 12582928 | tf_op jit(solution)/shard_map/all_gather | solution.py:12
  138.9 76.3 %conditional.1 = (f32[3,256]{1,0:T(4,128)S(1)}, f32[256,3,128]{0,2,1:T(8,128)S(1)}) conditional(s32[]{:T(128)} %convert_element_type.52, () %tuple.13, (pred[256,8192]{1,0:T(8,128)(4,1)}, bf16[256,384]{1,0:T(8,128)(2,1)S(1)}, bf16[8192,768]{1,0:T(8,128)(2,1)}) %tuple.14), branch_computations={%region_4.5_spmd, %region_5.8_spmd} | conditional | flops 3305110784 | bytes 182143024 | solution.py:81
  138.9 16.2 %copy.25 = bf16[8192,768]{0,1:T(8,128)(2,1)} copy(bf16[8192,768]{1,0:T(8,128)(2,1)} %get-tuple-element.30) | data formatting | bytes 25165824 | tf_op jit(solution)/shard_map
  155.1 10.3 %fusion.42 = (bf16[8192,384]{0,1:T(8,128)(2,1)}, bf16[8192,384]{0,1:T(8,128)(2,1)}) fusion(bf16[8192,768]{0,1:T(8,128)(2,1)} %copy.25), kind=kLoop, calls=%fused_computation.57 | loop fusion | bytes 25165824 | tf_op jit(solution)/shard_map/split | solution.py:13
  165.4 0.1 copy.24
  165.6 0.0 copy-start.1
  165.6 14.7 %fusion = (f32[3,256]{1,0:T(4,128)S(1)}, f32[3,256,8192]{2,1,0:T(8,128)}) fusion(pred[256,8192]{1,0:T(8,128)(4,1)} %get-tuple-element.15, bf16[256,3,128]{0,2,1:T(8,128)(2,1)S(1)} %bitcast.43, bf16[8192,3,128]{0,2,1:T(8,128)(2,1)} %bitcast.41), kind=kOutput, calls=%fused_computation.2 | convolution fusion | flops 1629486336 | bytes 33754112 | tf_op jit(solution)/shard_map/cond/branch_1_fun/thd,shd->hts/dot_general | solution.py:65
  180.3 0.0 copy-done.1
  180.3 4.2 %convert_element_type.34 = f32[256,8192]{1,0:T(8,128)} convert(pred[256,8192]{1,0:T(8,128)(4,1)S(1)} %copy-done.1) | non-fusion elementwise | flops 2097152 | bytes 10485760 | tf_op jit(solution)/shard_map/cond/branch_1_fun/convert_element_type | solution.py:70
  184.5 16.3 %fusion.6 = f32[256,3,128]{2,0,1:T(8,128)S(1)} fusion(bf16[8192,3,128]{0,2,1:T(8,128)(2,1)} %bitcast.38, f32[3,256,8192]{2,1,0:T(8,128)} %get-tuple-element.35, f32[256,8192]{1,0:T(8,128)} %convert_element_type.34, f32[3,256]{1,0:T(4,128)S(1)} %broadcast_maximum_fusion, pred[256,8192]{1,0:T(8,128)(4,1)} %get-tuple-element.15), kind=kOutput, calls=%fused_computation.7 | convolution fusion | flops 1642070016 | bytes 42339328 | tf_op jit(solution)/shard_map/cond/branch_1_fun/hts,shd->thd/dot_general | solution.py:72
  200.9 0.2 copy.32
  201.0 14.2 %fusion.2 = f32[3,256]{1,0:T(4,128)S(1)} fusion(f32[3,256,8192]{2,1,0:T(8,128)} %get-tuple-element.35, f32[256,8192]{1,0:T(8,128)} %convert_element_type.34, f32[3,256]{1,0:T(4,128)S(1)} %broadcast_maximum_fusion, pred[256,8192]{1,0:T(8,128)(4,1)} %get-tuple-element.15), kind=kLoop, calls=%fused_computation.4 | loop fusion | flops 31456512 | bytes 35657728 | tf_op jit(solution)/shard_map/cond/branch_1_fun/reduce_sum | solution.py:71
  215.2 0.0 copy-done
  215.3 1.0 convolution_convert_fusion
  216.3 1.3 copy.35
  217.6 5.6 %all-to-all-start = ((bf16[8,256,384]{2,1,0:T(8,128)(2,1)}), bf16[8,256,384]{2,1,0:T(8,128)(2,1)}, u32[]{:S(2)}, u32[]{:S(2)}) async-start(bf16[8,256,384]{2,1,0:T(8,128)(2,1)} %bitcast.39), calls=%async_computation | async-start | bytes 3145728 | tf_op jit(solution)/shard_map/all_to_all | solution.py:23
  223.3 3.4 %convert_element_type.49 = f32[256,3072]{1,0:T(8,128)} convert(bf16[256,3072]{1,0:T(8,128)(2,1)} %param.8) | non-fusion elementwise | flops 786432 | bytes 4718592 | tf_op jit(solution)/shard_map/convert_element_type | solution.py:32
  226.7 17.2 %all-to-all-done = bf16[8,256,384]{2,1,0:T(8,128)(2,1)} async-done(((bf16[8,256,384]{2,1,0:T(8,128)(2,1)}), bf16[8,256,384]{2,1,0:T(8,128)(2,1)}, u32[]{:S(2)}, u32[]{:S(2)}) %all-to-all-start) | async-done | bytes 1572896 | tf_op jit(solution)/shard_map/all_to_all | solution.py:23
  243.9 1.7 convert_reduce_fusion
  245.6 1.7 add_convert_fusion.1
  (8 shorter events, 0.1 us)
Async XLA Ops:
  6.5 208.7 %copy-start = (bf16[384,3072]{1,0:T(8,128)(2,1)S(1)}, bf16[384,3072]{1,0:T(8,128)(2,1)}, u32[]{:S(2)}) copy-start(bf16[384,3072]{1,0:T(8,128)(2,1)} %param.11) | copy-start | bytes 7077892
  6.5 3.8 %copy-start.3 = (f32[1,3,3072]{2,0,1:T(1,128)S(1)}, f32[1,3,3072]{2,0,1:T(1,128)}, u32[]{:S(2)}) copy-start(f32[1,3,3072]{2,0,1:T(1,128)} %param.9) | copy-start | bytes 110596
  6.5 132.3 %all-gather.2.cloned.1.call-start = ((), (), s32[]{:S(2)}) async-start(), calls=%async_computation.1 | async-start | bytes 12976128 | tf_op jit(solution)/shard_map/all_gather | solution.py:12
  6.5 3.9 %copy-start.2 = (bf16[256,3072]{1,0:T(8,128)(2,1)S(1)}, bf16[256,3072]{1,0:T(8,128)(2,1)}, u32[]{:S(2)}) copy-start(bf16[256,3072]{1,0:T(8,128)(2,1)} %param.8) | copy-start | bytes 4718596
  13.2 4.3 %copy-start.4 = (s32[32]{0:T(128)S(1)}, s32[32]{0:T(128)}, u32[]{:S(2)}) copy-start(s32[32]{0:T(128)} %param.13) | copy-start | bytes 388
  165.6 14.7 %copy-start.1 = (pred[256,8192]{1,0:T(8,128)(4,1)S(1)}, pred[256,8192]{1,0:T(8,128)(4,1)}, u32[]{:S(2)}) copy-start(pred[256,8192]{1,0:T(8,128)(4,1)} %get-tuple-element.15) | copy-start | bytes 6291460 | tf_op jit(solution)/shard_map/cond
  217.6 26.3 %all-to-all-start = ((bf16[8,256,384]{2,1,0:T(8,128)(2,1)}), bf16[8,256,384]{2,1,0:T(8,128)(2,1)}, u32[]{:S(2)}, u32[]{:S(2)}) async-start(bf16[8,256,384]{2,1,0:T(8,128)(2,1)} %bitcast.39), calls=%async_computation | async-start | bytes 3145728 | tf_op jit(solution)/shard_map/all_to_all | solution.py:23
Sparse Core Ops, SparseCore 0:
  16.9 121.9 all-gather.1
where the time goes:
time: 255 us; the launch traced here: 254 us
  waiting for transfers between devices  130 us (51%)
  matrix products  45 us (18%)
  other arithmetic  30.8 us (12%)
  local copies, waits for them, and re-layouts  28.3 us (11%)
  between operations  14.2 us (6%)
  starting transfers between devices  5.65 us (2%)
    all_gather x1, waiting for transfers between devices, side_by_side(): result = lax.all_gather(both, axis, axis=dim, tiled=True)  113 us
    all_to_all x1, waiting for transfers between devices, sent_and_summed(): lax.all_to_all(tiles, axis, split_axis=0, concat_axis=0, tiled=True)  17.2 us
    another operation x2, local copies, waits for them, and re-layouts  16.4 us
    dot_general x1, matrix products, update(): jnp.einsum('hts,shd->thd', weight.astype(jnp.bfloat16), value_heads, pref...  16.3 us
    dot_general x1, matrix products, update(): jnp.einsum('thd,shd->hts', query_heads, key_heads, preferred_element_type...  14.7 us
    reduce_sum x1, other arithmetic, update(): total = jnp.sum(weight, axis=-1)  14.2 us
    split x1, local copies, waits for them, and re-layouts, side_by_side(): jnp.split(result, [sum(widths[:k]) for k in range(1, len(widths))], axis=...  10.3 us
    all_to_all x1, starting transfers between devices, sent_and_summed(): lax.all_to_all(tiles, axis, split_axis=0, concat_axis=0, tiled=True)  5.65 us
  transfers between devices with their start and end apart: 2, of which 2 were waited for; matrix products, arithmetic and copies ran while one was open for 5% of the time, Pallas kernels for 0%

commit v1 on v0

v1 whole, which is shorter than its diff:
```python
import jax
import jax.numpy as jnp
from jax import lax
from jax.experimental import pallas as pl
from jax.experimental.pallas import tpu as pltpu
from jax.sharding import PartitionSpec as P

HS = 128
TOK = 256
NZ, NY, NX = 8, 4, 4
NEG = -1e30
LOG2E = 1.4426950408889634
HALF = TOK // 2


def rem(a, b):
    return lax.rem(a, jnp.int32(b))


def div(a, b):
    return lax.div(a, jnp.int32(b))


def kernel(
    lat_hbm, mod_hbm, wqkv_hbm, wout_hbm, mask_ref, len_ref, out_ref,
    lat, mod, adapted, wkv, wq, kvsend, qsend, kv, q, acc, mx, sm, attsend, att, wcol,
    in_sem, wkv_sem, kvs_sem, qs_sem, kv_sem, q_sem, b_sem, c_sem, att_sem, x_sem, wos_sem, wor_sem,
):
    t_id = lax.axis_index("tm")
    z, y = div(t_id, NY), rem(t_id, NY)
    m = lax.axis_index("mp")
    c = lax.axis_index("dec")
    yp, ym, y2 = rem(y + 1, NY), rem(y + NY - 1, NY), rem(y + 2, NY)
    xp, xm, x2 = rem(m + 1, NX), rem(m + NX - 1, NX), rem(m + 2, NX)
    width = wout_hbm.shape[0]
    row_core = div(z, 4)
    row_u = 3 * row_core + rem(z, 4)
    active = rem(z, 4) != 3

    def at(z_=z, y_=y, m_=m, c_=c):
        return {"tm": z_ * NY + y_, "mp": m_, "dec": c_}

    def remote(src, dst, ssem, rsem, device):
        return pltpu.make_async_remote_copy(
            src_ref=src, dst_ref=dst, send_sem=ssem, recv_sem=rsem,
            device_id=device, device_id_type=pl.DeviceIdType.MESH,
        )

    lat_copy = pltpu.make_async_copy(lat_hbm, lat, in_sem.at[0])
    mod_copy = pltpu.make_async_copy(mod_hbm.at[0], mod, in_sem.at[1])
    lat_copy.start()
    mod_copy.start()

    def weight_copy(k, part):
        cols = pl.ds(pl.multiple_of(k * HS, HS), HS)
        return pltpu.make_async_copy(
            wqkv_hbm.at[1 + part, :, cols], wkv.at[k, :, pl.ds(part * HS, HS)], wkv_sem.at[k, part]
        )

    for k in range(3):
        for part in range(2):
            weight_copy(k, part).start()
    wq_copy = pltpu.make_async_copy(wqkv_hbm.at[0], wq, in_sem.at[2])
    wq_copy.start()
    own_cols = pl.ds(pl.multiple_of((2 * m + c) * width, HS), width)
    own_rows = pl.ds(pl.multiple_of(c * width, HS), width)
    wout_copy = pltpu.make_async_copy(wout_hbm.at[:, own_cols], wcol.at[m, own_rows, :], in_sem.at[3])
    wout_copy.start()

    barrier = pltpu.get_barrier_semaphore()
    partners = [at(c_=1 - c), at(y_=yp), at(y_=ym)]
    for dz in range(1, NZ):
        for cc in range(2):
            partners.append(at(z_=rem(z + dz, NZ), c_=jnp.int32(cc)))
    for dx in range(1, NX):
        for cc in range(2):
            partners.append(at(m_=rem(m + dx, NX), c_=jnp.int32(cc)))
    for device in partners:
        pl.semaphore_signal(barrier, inc=1, device_id=device, device_id_type=pl.DeviceIdType.MESH)

    lat_copy.wait()
    mod_copy.wait()
    rows = 16

    @pl.loop(0, TOK // rows)
    def _(r):
        block = pl.ds(pl.multiple_of(r * rows, rows), rows)
        wide = lat[block, :].astype(jnp.float32)
        centred = wide - jnp.mean(wide, axis=-1, keepdims=True)
        var = jnp.mean(centred * centred, axis=-1, keepdims=True)
        normed = centred * lax.rsqrt(var + 1e-06)
        adapted[block, :] = (normed * (1.0 + mod[1:2, :]) + mod[0:1, :]).astype(jnp.bfloat16)

    pl.semaphore_wait(barrier, len(partners))

    def wout_sends():
        copies = []
        for dx in range(NX):
            for dc in range(2):
                if dx == 0 and dc == 0:
                    continue
                m_, c_ = rem(m + dx, NX), rem(c + dc, 2)
                cols = pl.ds(pl.multiple_of((2 * m_ + c_) * width, HS), width)
                copies.append(remote(
                    wout_hbm.at[:, cols], wcol.at[m, own_rows, :],
                    wos_sem.at[dx, dc], wor_sem.at[dx, dc], at(m_=m_, c_=c_),
                ))
        return copies

    for copy in wout_sends():
        copy.start()

    def piece(s, p, start=0, size=TOK):
        return kv.at[s, pl.ds(pl.multiple_of(p * TOK + start, HALF), size), :]

    q_core = rem(div(z + 1, 2), 2)
    slab_core = rem(z, 2)

    def kv_remote(k):
        return remote(kvsend.at[k], piece(z, y), kvs_sem.at[k], kv_sem.at[z, y, 0], at(z_=4 * c + k, c_=slab_core))

    def q_remote(k):
        return remote(qsend.at[k], q.at[div(z, 2)], qs_sem.at[k], q_sem.at[div(z, 2)], at(z_=4 * c + k, c_=q_core))

    @pl.loop(0, 3)
    def _(k):
        weight_copy(k, 0).wait()
        weight_copy(k, 1).wait()
        made = jnp.dot(adapted[...], wkv[k], preferred_element_type=jnp.float32).astype(jnp.bfloat16)
        here = (4 * c + k == z) & (slab_core == c)

        @pl.when(here)
        def _():
            kv[z, pl.ds(pl.multiple_of(y * TOK, TOK), TOK), :] = made

        @pl.when(jnp.logical_not(here))
        def _():
            kvsend[k] = made
            kv_remote(k).start()

    wq_copy.wait()
    made_q = jnp.dot(adapted[...], wq[...], preferred_element_type=jnp.float32) * (LOG2E / HS**0.5)
    made_q = made_q.astype(jnp.bfloat16)
    for k in range(3):
        here = (4 * c + k == z) & (q_core == c)
        one = made_q[:, k * HS:(k + 1) * HS]

        @pl.when(here)
        def _():
            q[div(z, 2)] = one

        @pl.when(jnp.logical_not(here))
        def _():
            qsend[k] = one
            q_remote(k).start()

    def order(t):
        return rem(z + (1 - 2 * rem(t, 2)) * div(t + 1, 2) + NZ, NZ)

    def group_row(k):
        return 2 * k + rem(k + c, 2)

    def kv_wait(s, p, half=0, size=TOK):
        start = half * HALF if size == HALF else 0
        ref = piece(s, p, start, size)
        remote(ref, ref, b_sem.at[s, 0], kv_sem.at[s, p, half], at(c_=1 - c)).wait_recv()

    def hop(s, p, slot, device, half=None):
        start, size = (0, TOK) if half is None else (half * HALF, HALF)
        ref = piece(s, p, start, size)
        return remote(ref, ref, b_sem.at[s, slot], kv_sem.at[s, p, half or 0], device)

    def hops(s):
        up, down, across = at(y_=yp), at(y_=ym), at(c_=1 - c)
        return [
            hop(s, y, 0, up), hop(s, y, 1, down), hop(s, y, 2, across),
            hop(s, ym, 3, up, 0), hop(s, ym, 4, across),
            hop(s, yp, 5, down, 1), hop(s, yp, 6, across),
            hop(s, y2, 7, across),
        ]

    def tile(k, s):
        group = group_row(k) * NY + y
        lane = lax.broadcasted_iota(jnp.int32, (1, TOK), 1)
        parts = []
        for p in range(NY):
            key_group = s * NY + p
            limit = jnp.where(mask_ref[group, key_group] == 1, len_ref[key_group], 0)
            parts.append(jnp.where(lane < limit, 0.0, NEG).astype(jnp.float32))
        bias = jnp.concatenate(parts, axis=1)
        score = lax.dot_general(
            q[k], kv[s, :, 0:HS], (((1,), (1,)), ((), ())), preferred_element_type=jnp.float32
        ) + bias
        old = mx[k]
        new = jnp.maximum(old, jnp.max(score, axis=-1, keepdims=True))
        keep = jnp.exp2(old - new)
        weight = jnp.exp2(score - new[:, 0:1])
        mx[k] = new
        sm[k] = sm[k] * keep + jnp.sum(weight, axis=-1, keepdims=True)
        acc[k] = acc[k] * keep + jnp.dot(
            weight.astype(jnp.bfloat16), kv[s, :, HS:2 * HS], preferred_element_type=jnp.float32
        )

    def att_piece(x, u, half=None):
        start, size = (0, TOK) if half is None else (half * HALF, HALF)
        return att.at[x, pl.ds(start, size), pl.ds(pl.multiple_of(u * HS, HS), HS)]

    def att_remote(k):
        return remote(
            attsend.at[k], att_piece(m, row_u), c_sem.at[k], att_sem.at[m, row_u, 0],
            at(z_=group_row(k), c_=row_core),
        )

    def q_here(k):
        return (group_row(k) == z) & (row_core == c)

    @pl.when(active)
    def _():
        mx[...] = jnp.full(mx.shape, NEG, jnp.float32)
        sm[...] = jnp.zeros(sm.shape, jnp.float32)
        acc[...] = jnp.zeros(acc.shape, jnp.float32)

        @pl.loop(0, NZ + 3)
        def _(t):
            @pl.when(t < NZ)
            def _():
                s = order(t)

                @pl.when(rem(s, 2) == c)
                def _():
                    @pl.when(jnp.logical_not((t == 0) & (row_core == c)))
                    def _():
                        kv_wait(s, y)

                    for copy in hops(s)[0:3]:
                        copy.start()

            @pl.when((t >= 1) & (t < NZ + 1))
            def _():
                s = order(t - 1)

                @pl.when(rem(s, 2) == c)
                def _():
                    kv_wait(s, ym)
                    for copy in hops(s)[3:5]:
                        copy.start()
                    kv_wait(s, yp)
                    for copy in hops(s)[5:7]:
                        copy.start()

            @pl.when((t >= 2) & (t < NZ + 2))
            def _():
                s = order(t - 2)

                @pl.when(rem(s, 2) == c)
                def _():
                    kv_wait(s, y2, 0, HALF)
                    kv_wait(s, y2, 1, HALF)
                    hops(s)[7].start()

            @pl.when(t >= 3)
            def _():
                s = order(t - 3)

                @pl.when(rem(s, 2) != c)
                def _():
                    for p in range(NY):
                        kv_wait(s, jnp.int32(p))

                @pl.when(t == 3)
                def _():
                    for k in range(4):
                        @pl.when(jnp.logical_not(q_here(jnp.int32(k))))
                        def _():
                            remote(q.at[k], q.at[k], c_sem.at[k], q_sem.at[k], at(c_=1 - c)).wait_recv()

                @pl.loop(0, 4)
                def _(k):
                    @pl.when(s <= group_row(k))
                    def _():
                        tile(k, s)

                    @pl.when(t == NZ + 2)
                    def _():
                        done = (acc[k] / sm[k]).astype(jnp.bfloat16)

                        @pl.when(q_here(k))
                        def _():
                            att[m, :, pl.ds(pl.multiple_of(row_u * HS, HS), HS)] = done

                        @pl.when(jnp.logical_not(q_here(k)))
                        def _():
                            attsend[k] = done
                            att_remote(k).start()

    def att_wait(x, u, half=None):
        ref = att_piece(x, u, half)
        remote(ref, ref, x_sem.at[0, 0], att_sem.at[x, u, half or 0], at(c_=1 - c)).wait_recv()

    def att_hop(x, u, k, slot, device, half=None):
        ref = att_piece(x, u, half)
        return remote(ref, ref, x_sem.at[k, slot], att_sem.at[x, u, half or 0], device)

    def att_hops(k):
        u = 3 * c + k
        up, down, across = at(m_=xp), at(m_=xm), at(c_=1 - c)
        return [
            att_hop(m, u, k, 0, up), att_hop(m, u, k, 1, down), att_hop(m, u, k, 2, across),
            att_hop(xm, u, k, 3, up, 0), att_hop(xm, u, k, 4, across),
            att_hop(xp, u, k, 5, down, 1), att_hop(xp, u, k, 6, across),
            att_hop(x2, u, k, 7, across),
        ]

    @pl.loop(0, 3)
    def _(k):
        @pl.when(jnp.logical_not((4 * c + k == z) & (q_core == c)))
        def _():
            att_wait(m, 3 * c + k)

        for copy in att_hops(k)[0:3]:
            copy.start()

    @pl.loop(0, 3)
    def _(k):
        att_wait(xm, 3 * c + k)
        for copy in att_hops(k)[3:5]:
            copy.start()
        att_wait(xp, 3 * c + k)
        for copy in att_hops(k)[5:7]:
            copy.start()

    @pl.loop(0, 3)
    def _(k):
        att_wait(x2, 3 * c + k, 0)
        att_wait(x2, 3 * c + k, 1)
        att_hops(k)[7].start()

    wout_copy.wait()
    for copy in wout_sends():
        copy.wait_recv()
    for x in range(NX):
        for k in range(3):
            att_wait(jnp.int32(x), 3 * (1 - c) + k)

    branch = jnp.dot(att[0], wcol[0], preferred_element_type=jnp.float32)
    for x in range(1, NX):
        branch += jnp.dot(att[x], wcol[x], preferred_element_type=jnp.float32)
    wide = lat[:, own_cols].astype(jnp.float32)
    out_ref[...] = (wide + mod[2:3, own_cols] * branch).astype(jnp.bfloat16)

    for copy in wout_sends():
        copy.wait_send()

    @pl.loop(0, 3)
    def _(k):
        @pl.when(jnp.logical_not((4 * c + k == z) & (slab_core == c)))
        def _():
            kv_remote(k).wait_send()

        @pl.when(jnp.logical_not((4 * c + k == z) & (q_core == c)))
        def _():
            q_remote(k).wait_send()

        for copy in att_hops(k):
            copy.wait_send()

    @pl.when(active)
    def _():
        @pl.loop(0, NZ)
        def _(s):
            @pl.when(rem(s, 2) == c)
            def _():
                for copy in hops(s):
                    copy.wait_send()

        @pl.loop(0, 4)
        def _(k):
            @pl.when(jnp.logical_not(q_here(k)))
            def _():
                att_remote(k).wait_send()


def shards(latents, modulation, w_qkv, w_out, block_mask, lengths):
    tok, d = latents.shape
    width = w_out.shape[0]
    dma = pltpu.SemaphoreType.DMA
    vmem = pltpu.VMEM
    bf16, f32 = jnp.bfloat16, jnp.float32
    anywhere = pl.BlockSpec(memory_space=pl.ANY)
    scalars = pl.BlockSpec(memory_space=pltpu.SMEM)
    return pl.pallas_call(
        kernel,
        out_shape=jax.ShapeDtypeStruct((tok, width), bf16),
        in_specs=[anywhere] * 4 + [scalars] * 2,
        out_specs=pl.BlockSpec(memory_space=pltpu.VMEM),
        scratch_shapes=[
            vmem((tok, d), bf16), vmem((3, d), f32), vmem((tok, d), bf16),
            vmem((3, d, 2 * HS), bf16), vmem((d, width), bf16),
            vmem((3, tok, 2 * HS), bf16), vmem((3, tok, HS), bf16),
            vmem((NZ, NY * tok, 2 * HS), bf16), vmem((4, tok, HS), bf16),
            vmem((4, tok, HS), f32), vmem((4, tok, HS), f32), vmem((4, tok, HS), f32),
            vmem((4, tok, HS), bf16), vmem((NX, tok, 6 * HS), bf16), vmem((NX, 2 * width, width), bf16),
            dma((4,)), dma((3, 2)), dma((3,)), dma((3,)), dma((NZ, NY, 2)), dma((4,)),
            dma((NZ, 8)), dma((4,)), dma((NX, 6, 2)), dma((3, 8)), dma((NX, 2)), dma((NX, 2)),
        ],
        compiler_params=pltpu.CompilerParams(
            collective_id=0, has_side_effects=True, vmem_limit_bytes=60 * 1024 * 1024
        ),
        name="attention_sublayer",
    )(latents, modulation, w_qkv, w_out, block_mask, lengths)


def solution(mesh):
    return jax.shard_map(
        shards,
        mesh=mesh,
        in_specs=(
            P("tm", None),
            P("tm", None, None),
            P(None, None, ("mp", "dec")),
            P(("mp", "dec"), None),
            P(),
            P(),
        ),
        out_specs=P("tm", ("mp", "dec")),
        check_vma=False,
    )
```

time: 255 us -> 79.1 us (0.31)
  waiting for transfers between devices: 130 us -> 0 us
  Pallas kernels: 0 us -> 75.8 us
  matrix products: 45 us -> 0 us
  other arithmetic: 30.8 us -> 0 us
  local copies, waits for them, and re-layouts: 28.3 us -> 3.02 us
  between operations: 14.2 us -> 0.01 us
  starting transfers between devices: 5.65 us -> 0 us
    all_gather x1 -> x0, waiting for transfers between devices: 113 us -> none  [side_by_side(): result = lax.all_gather(both, axis, axis=dim, tiled=True)]
    pallas_call x0 -> x1, Pallas kernels: none -> 75.8 us  [shards(): pl.pallas_call(kernel, out_shape=jax.ShapeDtypeStruct((tok, width), bf16)...]
    dot_general x7 -> x0, matrix products: 45 us -> none  [the longest x1 16.3 us: update(): jnp.einsum('hts,shd->thd', weight.astype(jnp.bfloat16), value_heads, pref...]
    reduce_sum x5 -> x0, other arithmetic: 19.9 us -> none  [the longest x1 14.2 us: update(): total = jnp.sum(weight, axis=-1)]
    all_to_all x1 -> x0, waiting for transfers between devices: 17.2 us -> none  [sent_and_summed(): lax.all_to_all(tiles, axis, split_axis=0, concat_axis=0, tiled=True)]
    another operation x2 -> x0, local copies, waits for them, and re-layouts: 16.4 us -> none
    split x1 -> x0, local copies, waits for them, and re-layouts: 10.3 us -> none  [side_by_side(): jnp.split(result, [sum(widths[:k]) for k in range(1, len(widths))], axis=...]
    convert_element_type x5 -> x0, other arithmetic: 10.1 us -> none  [the longest x1 4.22 us: update(): allowed[None, :, :].astype(jnp.float32)]
  transfers between devices with their start and end apart: 2 -> 0, of which waited for: 2 -> 0; matrix products, arithmetic and copies ran while one was open for 5% -> 0% of each run, Pallas kernels for 0% -> 0%
where the time goes in v1:
time: 79.1 us; the launch traced here: 78.9 us
  Pallas kernels  75.8 us (96%)
  local copies, waits for them, and re-layouts  3.02 us (4%)
    pallas_call x1, Pallas kernels, shards(): pl.pallas_call(kernel, out_shape=jax.ShapeDtypeStruct((tok, width), bf16)...  75.8 us
    unnamed x2, local copies, waits for them, and re-layouts  3.02 us

profile of v1, /device:TPU:1, one launch (start us, length us, event | category | flops | bytes accessed | tf_op | source)
XLA Modules:
  0.0 78.9 jit_solution(10186691759439392541)
XLA Ops:
  0.0 1.4 %copy.7.mod_hbm = f32[1,3,3072]{2,1,0:T(4,128)} copy(f32[1,3,3072]{2,0,1:T(1,128)} %param.7) | data formatting | bytes 73728 | tf_op args[1]
  1.4 75.8 %attention_sublayer.1 = bf16[256,384]{1,0:T(8,128)(2,1)} custom-call(bf16[256,3072]{1,0:T(8,128)(2,1)} %lat_hbm.1, f32[1,3,3072]{2,1,0:T(4,128)} %copy.7.mod_hbm, bf16[3,3072,384]{2,1,0:T(8,128)(2,1)} %wqkv_hbm.1, bf16[384,3072]{1,0:T(8,128)(2,1)} %wout_hbm.1, s32[32,32]{1,0:T(8,128)} %mask_ref.1, s32[32]{0:T(128)} %len_ref.1), custom_call_target="tpu_custom_call" | custom-call | tf_op jit(solution)/shard_map/attention_sublayer/pallas_call | solution.py:391
  77.2 1.6 %copy.9 = bf16[256,384]{1,0:T(8,128)(2,1)} copy(bf16[256,384]{1,0:T(8,128)(2,1)} %attention_sublayer.1) | data formatting | bytes 393216

commit v2 on v1

v2 whole, which is shorter than its diff:
```python
import jax
import jax.numpy as jnp
from jax import lax
from jax.experimental import pallas as pl
from jax.experimental.pallas import tpu as pltpu
from jax.sharding import PartitionSpec as P

HS = 128
TOK = 256
NZ, NY, NX = 8, 4, 4
NEG = -1e30
LOG2E = 1.4426950408889634
HALF = TOK // 2
PAUSE = 2500


def rem(a, b):
    return lax.rem(a, jnp.int32(b))


def div(a, b):
    return lax.div(a, jnp.int32(b))


def kernel(
    lat_hbm, mod_hbm, wqkv_hbm, wout_hbm, mask_ref, len_ref, out_ref,
    lat, mod, adapted, wqkv, kvsend, qsend, kv, q, acc, mx, sm, attsend, att, wcol, branch,
    in_sem, w_sem, kvs_sem, qs_sem, kv_sem, q_sem, b_sem, c_sem, att_sem, x_sem, wos_sem, wor_sem,
):
    t_id = lax.axis_index("tm")
    z, y = div(t_id, NY), rem(t_id, NY)
    m = lax.axis_index("mp")
    c = lax.axis_index("dec")
    yp, ym, y2 = rem(y + 1, NY), rem(y + NY - 1, NY), rem(y + 2, NY)
    xp, xm, x2 = rem(m + 1, NX), rem(m + NX - 1, NX), rem(m + 2, NX)
    width = wout_hbm.shape[0]
    row_core = div(z, 4)
    row_u = 3 * row_core + rem(z, 4)
    active = rem(z, 4) != 3
    q_core = rem(div(z + 1, 2), 2)
    slab_core = rem(z, 2)

    rel = rem(z - 4 * c + NZ, NZ)
    first = jnp.where(rel == 1, 1, jnp.where((rel >= 2) & (rel <= 4), 2, 0))
    second = jnp.where(rel == 1, 0, jnp.where(rel == 5, 2, 1))

    def nearest(i):
        return jnp.where(i == 0, first, jnp.where(i == 1, second, 3 - first - second))

    def at(z_=z, y_=y, m_=m, c_=c):
        return {"tm": z_ * NY + y_, "mp": m_, "dec": c_}

    def remote(src, dst, ssem, rsem, device):
        return pltpu.make_async_remote_copy(
            src_ref=src, dst_ref=dst, send_sem=ssem, recv_sem=rsem,
            device_id=device, device_id_type=pl.DeviceIdType.MESH,
        )

    lat_copy = pltpu.make_async_copy(lat_hbm, lat, in_sem.at[0])
    mod_copy = pltpu.make_async_copy(mod_hbm, mod, in_sem.at[1])
    lat_copy.start()
    mod_copy.start()

    barrier = pltpu.get_barrier_semaphore()
    partners = [at(c_=1 - c), at(y_=yp), at(y_=ym)]
    for dz in range(1, NZ):
        for cc in range(2):
            partners.append(at(z_=rem(z + dz, NZ), c_=jnp.int32(cc)))
    for dx in range(1, NX):
        for cc in range(2):
            partners.append(at(m_=rem(m + dx, NX), c_=jnp.int32(cc)))
    for device in partners:
        pl.semaphore_signal(barrier, inc=1, device_id=device, device_id_type=pl.DeviceIdType.MESH)

    def weight_copy(k, part):
        cols = pl.ds(pl.multiple_of(k * HS, HS), HS)
        return pltpu.make_async_copy(
            wqkv_hbm.at[(part + 1) % 3, :, cols], wqkv.at[k, :, pl.ds(part * HS, HS)], w_sem.at[k, part]
        )

    for i in range(3):
        for part in range(3):
            weight_copy(nearest(i), part).start()
    own_cols = pl.ds(pl.multiple_of((2 * m + c) * width, HS), width)
    own_rows = pl.ds(pl.multiple_of(c * width, HS), width)
    wout_copy = pltpu.make_async_copy(wout_hbm.at[:, own_cols], wcol.at[m, own_rows, :], in_sem.at[2])
    wout_copy.start()

    mx[...] = jnp.full(mx.shape, NEG, jnp.float32)
    sm[...] = jnp.zeros(sm.shape, jnp.float32)
    acc[...] = jnp.zeros(acc.shape, jnp.float32)

    with jax.named_scope("load"):
        lat_copy.wait()
        mod_copy.wait()
    rows = 16

    @pl.loop(0, TOK // rows, unroll=4)
    def _(r):
        block = pl.ds(pl.multiple_of(r * rows, rows), rows)
        wide = lat[block, :].astype(jnp.float32)
        centred = wide - jnp.mean(wide, axis=-1, keepdims=True)
        var = jnp.mean(centred * centred, axis=-1, keepdims=True)
        normed = centred * lax.rsqrt(var + 1e-06)
        adapted[block, :] = (normed * (1.0 + mod[1]) + mod[0]).astype(jnp.bfloat16)

    with jax.named_scope("entry"):
        pl.semaphore_wait(barrier, len(partners))

    def wout_send(dx, dc):
        m_, c_ = rem(m + dx, NX), rem(c + dc, 2)
        cols = pl.ds(pl.multiple_of((2 * m_ + c_) * width, HS), width)
        return remote(
            wout_hbm.at[:, cols], wcol.at[m, own_rows, :],
            wos_sem.at[0], wor_sem.at[dx, dc], at(m_=m_, c_=c_),
        )

    others = [(dx, dc) for dx in range(NX) for dc in range(2) if (dx, dc) != (0, 0)]

    def piece(s, p, start=0, size=TOK):
        return kv.at[s, pl.ds(pl.multiple_of(p * TOK + start, HALF), size), :]

    def kv_remote(k):
        return remote(kvsend.at[k], piece(z, y), kvs_sem.at[k], kv_sem.at[z, y, 0], at(z_=4 * c + k, c_=slab_core))

    def q_remote(k):
        return remote(qsend.at[k], q.at[div(z, 2)], qs_sem.at[k], q_sem.at[div(z, 2)], at(z_=4 * c + k, c_=q_core))

    def kv_local(k):
        return (4 * c + k == z) & (slab_core == c)

    def q_local(k):
        return (4 * c + k == z) & (q_core == c)

    def send_phase(phase, i):
        k = nearest(i)
        away = rem(4 * c + k - z + NZ, NZ)
        far = jnp.maximum(jnp.minimum(away, NZ - away), 1)

        @pl.when((far == phase) & jnp.logical_not(kv_local(k)))
        def _():
            kv_remote(k).start()

        @pl.when((jnp.maximum(far - 1, 1) == phase) & jnp.logical_not(q_local(k)))
        def _():
            q_remote(k).start()

    def send_rest(phase):
        @pl.loop(0, 3)
        def _(i):
            send_phase(phase, i)

    @pl.loop(0, 3)
    def _(i):
        k = nearest(i)
        with jax.named_scope("weights"):
            for part in range(3):
                weight_copy(k, part).wait()
        made = jnp.dot(adapted[...], wqkv[k], preferred_element_type=jnp.float32)
        kvsend[k] = made[:, 0:2 * HS].astype(jnp.bfloat16)
        qsend[k] = (made[:, 2 * HS:3 * HS] * (LOG2E / HS**0.5)).astype(jnp.bfloat16)

        @pl.when(kv_local(k))
        def _():
            kv[z, pl.ds(pl.multiple_of(y * TOK, TOK), TOK), :] = kvsend[k]

        @pl.when(q_local(k))
        def _():
            q[div(z, 2)] = qsend[k]

        send_phase(1, i)

        @pl.when(i == 0)
        def _():
            for pair in others:
                wout_send(*pair).start()

    def order(t):
        return rem(z + (1 - 2 * rem(t, 2)) * div(t + 1, 2) + NZ, NZ)

    def group_row(k):
        return 2 * k + rem(k + c, 2)

    def q_here(k):
        return (group_row(k) == z) & (row_core == c)

    def kv_wait(s, p, half=0, size=TOK):
        start = half * HALF if size == HALF else 0
        ref = piece(s, p, start, size)
        remote(ref, ref, b_sem.at[0], kv_sem.at[s, p, half], at(c_=1 - c)).wait_recv()

    def hop(s, slot):
        p, device, half = (
            (y, at(y_=yp), None), (y, at(y_=ym), None), (y, at(c_=1 - c), None),
            (ym, at(y_=yp), 0), (ym, at(c_=1 - c), None),
            (yp, at(y_=ym), 1), (yp, at(c_=1 - c), None),
            (y2, at(c_=1 - c), None),
        )[slot]
        start, size = (0, TOK) if half is None else (half * HALF, HALF)
        ref = piece(s, p, start, size)
        return remote(ref, ref, b_sem.at[0], kv_sem.at[s, p, half or 0], device)

    def relay(t, k):
        @pl.when((k == 0) & (t < NZ))
        def _():
            s = order(t)

            @pl.when(rem(s, 2) == c)
            def _():
                @pl.when(jnp.logical_not((t == 0) & (row_core == c)))
                def _():
                    with jax.named_scope("wait_z"):
                        kv_wait(s, y)

                for slot in range(3):
                    hop(s, slot).start()

        @pl.when((k == 1) & (t >= 1) & (t < NZ + 1))
        def _():
            s = order(t - 1)

            @pl.when(rem(s, 2) == c)
            def _():
                with jax.named_scope("wait_ym"):
                    kv_wait(s, ym)
                hop(s, 3).start()
                hop(s, 4).start()

        @pl.when((k == 2) & (t >= 1) & (t < NZ + 1))
        def _():
            s = order(t - 1)

            @pl.when(rem(s, 2) == c)
            def _():
                with jax.named_scope("wait_yp"):
                    kv_wait(s, yp)
                hop(s, 5).start()
                hop(s, 6).start()

        @pl.when((k == 3) & (t >= 2) & (t < NZ + 2))
        def _():
            s = order(t - 2)

            @pl.when(rem(s, 2) == c)
            def _():
                with jax.named_scope("wait_y2"):
                    kv_wait(s, y2, 0, HALF)
                    kv_wait(s, y2, 1, HALF)
                hop(s, 7).start()

        @pl.when((k == 0) & (t >= 3))
        def _():
            s = order(t - 3)

            @pl.when(rem(s, 2) != c)
            def _():
                with jax.named_scope("wait_core"):
                    for p in range(NY):
                        kv_wait(s, jnp.int32(p))

    def tile(k, s):
        group = group_row(k) * NY + y
        lane = lax.broadcasted_iota(jnp.int32, (1, TOK), 1)
        parts = []
        for p in range(NY):
            key_group = s * NY + p
            limit = jnp.where(mask_ref[group, key_group] == 1, len_ref[key_group], 0)
            parts.append(jnp.where(lane < limit, 0.0, NEG).astype(jnp.float32))
        bias = jnp.concatenate(parts, axis=1)
        score = lax.dot_general(
            q[k], kv[s, :, 0:HS], (((1,), (1,)), ((), ())), preferred_element_type=jnp.float32
        ) + bias
        old = mx[k]
        new = jnp.maximum(old, jnp.max(score, axis=-1, keepdims=True))
        keep = jnp.exp2(old - new)
        weight = jnp.exp2(score - new[:, 0:1])
        mx[k] = new
        total = weight[:, 0:HS]
        for i in range(1, NY * TOK // HS):
            total += weight[:, i * HS:(i + 1) * HS]
        sm[k] = sm[k] * keep + total
        acc[k] = acc[k] * keep + jnp.dot(
            weight.astype(jnp.bfloat16), kv[s, :, HS:2 * HS], preferred_element_type=jnp.float32
        )

    def att_piece(x, u, half=None):
        start, size = (0, TOK) if half is None else (half * HALF, HALF)
        return att.at[x, pl.ds(start, size), pl.ds(pl.multiple_of(u * HS, HS), HS)]

    def att_remote(k):
        return remote(
            attsend.at[k], att_piece(m, row_u), c_sem.at[k], att_sem.at[m, row_u, 0],
            at(z_=group_row(k), c_=row_core),
        )

    def compute(j, k):
        row = group_row(k)
        away = rem(row - z + NZ, NZ)
        rank = jnp.where(away <= 3, 2 * away, jnp.where(away == 4, NZ - 1, 2 * (NZ - away) - 1))
        begin = jnp.maximum(rank - 2, 0)
        last = begin
        for i in range(NZ):
            last = jnp.where((order(jnp.int32(i)) <= row) & (i > last), i, last)

        @pl.when((j == begin) & jnp.logical_not(q_here(k)))
        def _():
            with jax.named_scope("wait_q"):
                remote(q.at[k], q.at[k], c_sem.at[k], q_sem.at[k], at(c_=1 - c)).wait_recv()

        @pl.when(j >= begin)
        def _():
            @pl.loop(jnp.where(j == begin, 0, j), j + 1)
            def _(i):
                s = order(i)

                @pl.when(s <= row)
                def _():
                    with jax.named_scope("tile"):
                        tile(k, s)

        @pl.when(j == last)
        def _():
            done = (acc[k] / jnp.sum(sm[k], axis=-1, keepdims=True)).astype(jnp.bfloat16)

            @pl.when(q_here(k))
            def _():
                att[m, :, pl.ds(pl.multiple_of(row_u * HS, HS), HS)] = done

            @pl.when(jnp.logical_not(q_here(k)))
            def _():
                attsend[k] = done
                att_remote(k).start()

    @pl.when(active)
    def _():
        @pl.loop(0, NZ + 3)
        def _(t):
            @pl.loop(0, 4)
            def _(k):
                relay(t, k)

                @pl.when((t == 0) & (k == 0))
                def _():
                    pl.delay(PAUSE)
                    send_rest(2)

                @pl.when((t == 2) & (k == 2))
                def _():
                    send_rest(3)

                @pl.when((t == 3) & (k == 1))
                def _():
                    send_rest(4)

                @pl.when(t >= 3)
                def _():
                    compute(t - 3, k)

    @pl.when(jnp.logical_not(active))
    def _():
        pl.delay(PAUSE)
        send_rest(2)
        pl.delay(2 * PAUSE)
        send_rest(3)

    def att_wait(x, u, half=None):
        ref = att_piece(x, u, half)
        remote(ref, ref, x_sem.at[0], att_sem.at[x, u, half or 0], at(c_=1 - c)).wait_recv()

    def att_hop(k, slot):
        u = 3 * c + k
        x, device, half = (
            (m, at(m_=xp), None), (m, at(m_=xm), None), (m, at(c_=1 - c), None),
            (xm, at(m_=xp), 0), (xm, at(c_=1 - c), None),
            (xp, at(m_=xm), 1), (xp, at(c_=1 - c), None),
            (x2, at(c_=1 - c), None),
        )[slot]
        ref = att_piece(x, u, half)
        return remote(ref, ref, x_sem.at[0], att_sem.at[x, u, half or 0], device)

    def project(x, core):
        cols = pl.ds(pl.multiple_of(core * width, HS), width)
        with jax.named_scope("project"):
            return jnp.dot(att[x, :, cols], wcol[x, cols, :], preferred_element_type=jnp.float32)

    @pl.loop(0, 3)
    def _(k):
        @pl.when(jnp.logical_not(q_local(k)))
        def _():
            with jax.named_scope("wait_att"):
                att_wait(m, 3 * c + k)

        for slot in range(3):
            att_hop(k, slot).start()

    with jax.named_scope("wait_wout"):
        wout_copy.wait()
        for pair in others:
            wout_send(*pair).wait_recv()
    branch[...] = project(m, c)

    @pl.loop(0, 3)
    def _(k):
        with jax.named_scope("wait_xm"):
            att_wait(xm, 3 * c + k)
        for slot in (3, 4):
            att_hop(k, slot).start()
        with jax.named_scope("wait_xp"):
            att_wait(xp, 3 * c + k)
        for slot in (5, 6):
            att_hop(k, slot).start()

    def project_across(x):
        with jax.named_scope("wait_across"):
            for k in range(3):
                att_wait(x, 3 * (1 - c) + k)
        branch[...] += project(x, 1 - c)

    project_across(m)
    branch[...] += project(xm, c)
    branch[...] += project(xp, c)

    @pl.loop(0, 3)
    def _(k):
        with jax.named_scope("wait_x2"):
            att_wait(x2, 3 * c + k, 0)
            att_wait(x2, 3 * c + k, 1)
        att_hop(k, 7).start()

    project_across(xm)
    project_across(xp)
    branch[...] += project(x2, c)
    project_across(x2)

    with jax.named_scope("final"):
        wide = lat[:, own_cols].astype(jnp.float32)
        out_ref[...] = (wide + mod[2, :, own_cols] * branch[...]).astype(jnp.bfloat16)

    def all_left(ref, sem):
        remote(ref, ref, sem, wor_sem.at[0, 0], at(c_=1 - c)).wait_send()

    with jax.named_scope("leave"):
        all_left(wqkv.at[0, pl.ds(0, 7 * width), pl.ds(0, width)], wos_sem.at[0])
        all_left(adapted.at[:, pl.ds(0, 21 * HS)], x_sem.at[0])

    @pl.loop(0, 3)
    def _(k):
        @pl.when(jnp.logical_not(kv_local(k)))
        def _():
            kv_remote(k).wait_send()

        @pl.when(jnp.logical_not(q_local(k)))
        def _():
            q_remote(k).wait_send()

    @pl.when(active)
    def _():
        all_left(kv.at[pl.ds(0, 7)], b_sem.at[0])

        @pl.loop(0, 4)
        def _(k):
            @pl.when(jnp.logical_not(q_here(k)))
            def _():
                att_remote(k).wait_send()


def shards(latents, modulation, w_qkv, w_out, block_mask, lengths):
    tok, d = latents.shape
    width = w_out.shape[0]
    dma = pltpu.SemaphoreType.DMA
    vmem = pltpu.VMEM
    bf16, f32 = jnp.bfloat16, jnp.float32
    anywhere = pl.BlockSpec(memory_space=pl.ANY)
    scalars = pl.BlockSpec(memory_space=pltpu.SMEM)
    return pl.pallas_call(
        kernel,
        out_shape=jax.ShapeDtypeStruct((tok, width), bf16),
        in_specs=[anywhere] * 4 + [scalars] * 2,
        out_specs=pl.BlockSpec(memory_space=pltpu.VMEM),
        scratch_shapes=[
            vmem((tok, d), bf16), vmem((3, 1, d), f32), vmem((tok, d), bf16),
            vmem((3, d, 3 * HS), bf16), vmem((3, tok, 2 * HS), bf16), vmem((3, tok, HS), bf16),
            vmem((NZ, NY * tok, 2 * HS), bf16), vmem((4, tok, HS), bf16),
            vmem((4, tok, HS), f32), vmem((4, tok, HS), f32), vmem((4, tok, HS), f32),
            vmem((4, tok, HS), bf16), vmem((NX, tok, 6 * HS), bf16), vmem((NX, 2 * width, width), bf16),
            vmem((tok, width), f32),
            dma((3,)), dma((3, 3)), dma((3,)), dma((3,)), dma((NZ, NY, 2)), dma((4,)),
            dma((1,)), dma((4,)), dma((NX, 6, 2)), dma((1,)), dma((1,)), dma((NX, 2)),
        ],
        compiler_params=pltpu.CompilerParams(
            collective_id=0, has_side_effects=True, vmem_limit_bytes=60 * 1024 * 1024
        ),
        name="attention_sublayer",
    )(latents, jnp.transpose(modulation, (1, 0, 2)), w_qkv, w_out, block_mask, lengths)


def solution(mesh):
    return jax.shard_map(
        shards,
        mesh=mesh,
        in_specs=(
            P("tm", None),
            P("tm", None, None),
            P(None, None, ("mp", "dec")),
            P(("mp", "dec"), None),
            P(),
            P(),
        ),
        out_specs=P("tm", ("mp", "dec")),
        check_vma=False,
    )
```

time: 79.1 us -> 69.6 us (0.88)
  the two profiles are of different devices: /device:TPU:1 before, /device:TPU:193 now
where the time goes in v2:
time: 69.6 us; the launch traced here: 69.4 us
  Pallas kernels  67.8 us (97%)
  local copies, waits for them, and re-layouts  1.62 us (2%)
    pallas_call x1, Pallas kernels, shards(): pl.pallas_call(kernel, out_shape=jax.ShapeDtypeStruct((tok, width), bf16)...  67.8 us
    unnamed x1, local copies, waits for them, and re-layouts  1.62 us

profile of v2, /device:TPU:193, one launch (start us, length us, event | category | flops | bytes accessed | tf_op | source)
XLA Modules:
  0.0 69.4 jit_solution(10096910921386081462)
XLA Ops:
  0.0 67.8 %attention_sublayer.1 = bf16[256,384]{1,0:T(8,128)(2,1)} custom-call(bf16[256,3072]{1,0:T(8,128)(2,1)} %lat_hbm.1, f32[3,1,3072]{2,1,0:T(1,128)} %bitcast.1, bf16[3,3072,384]{2,1,0:T(8,128)(2,1)} %wqkv_hbm.1, bf16[384,3072]{1,0:T(8,128)(2,1)} %wout_hbm.1, s32[32,32]{1,0:T(8,128)} %mask_ref.1, s32[32]{0:T(128)} %len_ref.1), custom_call_target="tpu_custom_call" | custom-call | tf_op jit(solution)/shard_map/attention_sublayer/pallas_call | solution.py:475
  67.8 1.6 %copy.8 = bf16[256,384]{1,0:T(8,128)(2,1)} copy(bf16[256,384]{1,0:T(8,128)(2,1)} %attention_sublayer.1) | data formatting | bytes 393216

commit v3 on v2

--- a/solution.py
+++ b/solution.py
@@ -344,11 +344,11 @@
                     pl.delay(PAUSE)
                     send_rest(2)
 
-                @pl.when((t == 2) & (k == 2))
+                @pl.when((t == 3) & (k == 0))
                 def _():
                     send_rest(3)
 
-                @pl.when((t == 3) & (k == 1))
+                @pl.when((t == 4) & (k == 1))
                 def _():
                     send_rest(4)
 
@@ -360,7 +360,7 @@
     def _():
         pl.delay(PAUSE)
         send_rest(2)
-        pl.delay(2 * PAUSE)
+        pl.delay(5 * PAUSE // 2)
         send_rest(3)
 
     def att_wait(x, u, half=None):
@@ -474,7 +474,7 @@
     scalars = pl.BlockSpec(memory_space=pltpu.SMEM)
     return pl.pallas_call(
         kernel,
-        out_shape=jax.ShapeDtypeStruct((tok, width), bf16),
+        out_shape=pltpu.VMEM((tok, width), bf16),
         in_specs=[anywhere] * 4 + [scalars] * 2,
         out_specs=pl.BlockSpec(memory_space=pltpu.VMEM),
         scratch_shapes=[

time: 69.6 us -> 64.5 us (0.927)
  the two profiles are of different devices: /device:TPU:193 before, /device:TPU:1 now
where the time goes in v3:
time: 64.5 us; the launch traced here: 63.9 us
  Pallas kernels  63.2 us (98%)
  local copies, waits for them, and re-layouts  0.68 us (1%)
    pallas_call x1, Pallas kernels, shards(): pl.pallas_call(kernel, out_shape=pltpu.VMEM((tok, width), bf16), in_specs...  63.2 us

profile of v3, /device:TPU:1, one launch (start us, length us, event | category | flops | bytes accessed | tf_op | source)
XLA Modules:
  0.0 63.9 jit_solution(6972544706138861609)
XLA Ops:
  0.0 63.2 %attention_sublayer.1 = bf16[256,384]{1,0:T(8,128)(2,1)S(1)} custom-call(bf16[256,3072]{1,0:T(8,128)(2,1)} %lat_hbm.1, f32[3,1,3072]{2,1,0:T(1,128)} %bitcast.1, bf16[3,3072,384]{2,1,0:T(8,128)(2,1)} %wqkv_hbm.1, bf16[384,3072]{1,0:T(8,128)(2,1)} %wout_hbm.1, s32[32,32]{1,0:T(8,128)} %mask_ref.1, s32[32]{0:T(128)} %len_ref.1), custom_call_target="tpu_custom_call" | custom-call | tf_op jit(solution)/shard_map/attention_sublayer/pallas_call | solution.py:475
  63.3 0.7 %copy.8 = bf16[256,384]{1,0:T(8,128)(2,1)} copy(bf16[256,384]{1,0:T(8,128)(2,1)S(1)} %attention_sublayer.1) | data formatting | bytes 393216

commit v4 on v3

--- a/solution.py
+++ b/solution.py
@@ -16,6 +16,10 @@
 
 def rem(a, b):
     return lax.rem(a, jnp.int32(b))
+
+
+def wrap(a, b):
+    return jnp.where(a >= b, a - b, a)
 
 
 def div(a, b):
@@ -31,8 +35,8 @@
     z, y = div(t_id, NY), rem(t_id, NY)
     m = lax.axis_index("mp")
     c = lax.axis_index("dec")
-    yp, ym, y2 = rem(y + 1, NY), rem(y + NY - 1, NY), rem(y + 2, NY)
-    xp, xm, x2 = rem(m + 1, NX), rem(m + NX - 1, NX), rem(m + 2, NX)
+    yp, ym, y2 = wrap(y + 1, NY), wrap(y + NY - 1, NY), wrap(y + 2, NY)
+    xp, xm, x2 = wrap(m + 1, NX), wrap(m + NX - 1, NX), wrap(m + 2, NX)
     width = wout_hbm.shape[0]
     row_core = div(z, 4)
     row_u = 3 * row_core + rem(z, 4)
@@ -40,7 +44,7 @@
     q_core = rem(div(z + 1, 2), 2)
     slab_core = rem(z, 2)
 
-    rel = rem(z - 4 * c + NZ, NZ)
+    rel = wrap(z - 4 * c + NZ, NZ)
     first = jnp.where(rel == 1, 1, jnp.where((rel >= 2) & (rel <= 4), 2, 0))
     second = jnp.where(rel == 1, 0, jnp.where(rel == 5, 2, 1))
 
@@ -65,10 +69,10 @@
     partners = [at(c_=1 - c), at(y_=yp), at(y_=ym)]
     for dz in range(1, NZ):
         for cc in range(2):
-            partners.append(at(z_=rem(z + dz, NZ), c_=jnp.int32(cc)))
+            partners.append(at(z_=wrap(z + dz, NZ), c_=jnp.int32(cc)))
     for dx in range(1, NX):
         for cc in range(2):
-            partners.append(at(m_=rem(m + dx, NX), c_=jnp.int32(cc)))
+            partners.append(at(m_=wrap(m + dx, NX), c_=jnp.int32(cc)))
     for device in partners:
         pl.semaphore_signal(barrier, inc=1, device_id=device, device_id_type=pl.DeviceIdType.MESH)
 
@@ -108,7 +112,7 @@
         pl.semaphore_wait(barrier, len(partners))
 
     def wout_send(dx, dc):
-        m_, c_ = rem(m + dx, NX), rem(c + dc, 2)
+        m_, c_ = wrap(m + dx, NX), (1 - c if dc else c)
         cols = pl.ds(pl.multiple_of((2 * m_ + c_) * width, HS), width)
         return remote(
             wout_hbm.at[:, cols], wcol.at[m, own_rows, :],
@@ -134,7 +138,7 @@
 
     def send_phase(phase, i):
         k = nearest(i)
-        away = rem(4 * c + k - z + NZ, NZ)
+        away = wrap(4 * c + k - z + NZ, NZ)
         far = jnp.maximum(jnp.minimum(away, NZ - away), 1)
 
         @pl.when((far == phase) & jnp.logical_not(kv_local(k)))
@@ -176,10 +180,10 @@
                 wout_send(*pair).start()
 
     def order(t):
-        return rem(z + (1 - 2 * rem(t, 2)) * div(t + 1, 2) + NZ, NZ)
+        return wrap(z + jnp.where(rem(t, 2) == 1, NZ - div(t + 1, 2), div(t + 1, 2)), NZ)
 
     def group_row(k):
-        return 2 * k + rem(k + c, 2)
+        return 2 * k + (1 - c if k % 2 else c)
 
     def q_here(k):
         return (group_row(k) == z) & (row_core == c)
@@ -200,13 +204,12 @@
         ref = piece(s, p, start, size)
         return remote(ref, ref, b_sem.at[0], kv_sem.at[s, p, half or 0], device)
 
-    def relay(t, k):
-        @pl.when((k == 0) & (t < NZ))
-        def _():
-            s = order(t)
-
-            @pl.when(rem(s, 2) == c)
-            def _():
+    def relay(t, k, rows, mine):
+        if k == 0:
+            @pl.when((t < NZ) & mine[0])
+            def _():
+                s = rows[0]
+
                 @pl.when(jnp.logical_not((t == 0) & (row_core == c)))
                 def _():
                     with jax.named_scope("wait_z"):
@@ -215,48 +218,35 @@
                 for slot in range(3):
                     hop(s, slot).start()
 
-        @pl.when((k == 1) & (t >= 1) & (t < NZ + 1))
-        def _():
-            s = order(t - 1)
-
-            @pl.when(rem(s, 2) == c)
-            def _():
-                with jax.named_scope("wait_ym"):
-                    kv_wait(s, ym)
-                hop(s, 3).start()
-                hop(s, 4).start()
-
-        @pl.when((k == 2) & (t >= 1) & (t < NZ + 1))
-        def _():
-            s = order(t - 1)
-
-            @pl.when(rem(s, 2) == c)
-            def _():
-                with jax.named_scope("wait_yp"):
-                    kv_wait(s, yp)
-                hop(s, 5).start()
-                hop(s, 6).start()
-
-        @pl.when((k == 3) & (t >= 2) & (t < NZ + 2))
-        def _():
-            s = order(t - 2)
-
-            @pl.when(rem(s, 2) == c)
-            def _():
-                with jax.named_scope("wait_y2"):
-                    kv_wait(s, y2, 0, HALF)
-                    kv_wait(s, y2, 1, HALF)
-                hop(s, 7).start()
-
-        @pl.when((k == 0) & (t >= 3))
-        def _():
-            s = order(t - 3)
-
-            @pl.when(rem(s, 2) != c)
+            @pl.when((t >= 3) & jnp.logical_not(mine[3]))
             def _():
                 with jax.named_scope("wait_core"):
                     for p in range(NY):
-                        kv_wait(s, jnp.int32(p))
+                        kv_wait(rows[3], jnp.int32(p))
+
+        if k == 1:
+            @pl.when((t >= 1) & (t < NZ + 1) & mine[1])
+            def _():
+                with jax.named_scope("wait_ym"):
+                    kv_wait(rows[1], ym)
+                hop(rows[1], 3).start()
+                hop(rows[1], 4).start()
+
+        if k == 2:
+            @pl.when((t >= 1) & (t < NZ + 1) & mine[1])
+            def _():
+                with jax.named_scope("wait_yp"):
+                    kv_wait(rows[1], yp)
+                hop(rows[1], 5).start()
+                hop(rows[1], 6).start()
+
+        if k == 3:
+            @pl.when((t >= 2) & (t < NZ + 2) & mine[2])
+            def _():
+                with jax.named_scope("wait_y2"):
+                    kv_wait(rows[2], y2, 0, HALF)
+                    kv_wait(rows[2], y2, 1, HALF)
+                hop(rows[2], 7).start()
 
     def tile(k, s):
         group = group_row(k) * NY + y
@@ -293,14 +283,18 @@
             at(z_=group_row(k), c_=row_core),
         )
 
-    def compute(j, k):
+    def slot_steps(k, by_distance):
         row = group_row(k)
-        away = rem(row - z + NZ, NZ)
+        away = wrap(row - z + NZ, NZ)
         rank = jnp.where(away <= 3, 2 * away, jnp.where(away == 4, NZ - 1, 2 * (NZ - away) - 1))
         begin = jnp.maximum(rank - 2, 0)
         last = begin
-        for i in range(NZ):
-            last = jnp.where((order(jnp.int32(i)) <= row) & (i > last), i, last)
+        for i, s in enumerate(by_distance):
+            last = jnp.where((s <= row) & (i > last), i, last)
+        return row, begin, last
+
+    def compute(j, k, s_now, steps):
+        row, begin, last = steps
 
         @pl.when((j == begin) & jnp.logical_not(q_here(k)))
         def _():
@@ -311,7 +305,7 @@
         def _():
             @pl.loop(jnp.where(j == begin, 0, j), j + 1)
             def _(i):
-                s = order(i)
+                s = jnp.where(i == j, s_now, order(i))
 
                 @pl.when(s <= row)
                 def _():
@@ -333,28 +327,36 @@
 
     @pl.when(active)
     def _():
-        @pl.loop(0, NZ + 3)
-        def _(t):
-            @pl.loop(0, 4)
-            def _(k):
-                relay(t, k)
-
-                @pl.when((t == 0) & (k == 0))
-                def _():
-                    pl.delay(PAUSE)
-                    send_rest(2)
-
-                @pl.when((t == 3) & (k == 0))
-                def _():
-                    send_rest(3)
-
-                @pl.when((t == 4) & (k == 1))
-                def _():
-                    send_rest(4)
+        by_distance = [wrap(z + (NZ - (i + 1) // 2 if i % 2 else i // 2), NZ) for i in range(NZ)]
+        steps = [slot_steps(k, by_distance) for k in range(4)]
+
+        def step(t, earlier):
+            rows = (order(t),) + earlier
+            mine = [rem(s, 2) == c for s in rows]
+            for k in range(4):
+                relay(t, k, rows, mine)
+                if k == 0:
+                    @pl.when(t == 0)
+                    def _():
+                        pl.delay(PAUSE)
+                        send_rest(2)
+
+                    @pl.when(t == 3)
+                    def _():
+                        send_rest(3)
+
+                if k == 1:
+                    @pl.when(t == 4)
+                    def _():
+                        send_rest(4)
 
                 @pl.when(t >= 3)
                 def _():
-                    compute(t - 3, k)
+                    compute(t - 3, k, rows[3], steps[k])
+
+            return rows[:3]
+
+        lax.fori_loop(0, NZ + 3, step, (z, z, z))
 
     @pl.when(jnp.logical_not(active))
     def _():
@@ -457,8 +459,7 @@
     def _():
         all_left(kv.at[pl.ds(0, 7)], b_sem.at[0])
 
-        @pl.loop(0, 4)
-        def _(k):
+        for k in range(4):
             @pl.when(jnp.logical_not(q_here(k)))
             def _():
                 att_remote(k).wait_send()

time: 64.5 us -> 64.3 us (level)
  the two profiles are of different devices: /device:TPU:1 before, /device:TPU:233 now
where the time goes in v4:
time: 64.3 us; the launch traced here: 64.2 us
  Pallas kernels  63.5 us (99%)
  local copies, waits for them, and re-layouts  0.68 us (1%)
    pallas_call x1, Pallas kernels, shards(): pl.pallas_call(kernel, out_shape=pltpu.VMEM((tok, width), bf16), in_specs...  63.5 us

profile of v4, /device:TPU:233, one launch (start us, length us, event | category | flops | bytes accessed | tf_op | source)
XLA Modules:
  0.0 64.2 jit_solution(10256107364564562902)
XLA Ops:
  0.0 63.5 %attention_sublayer.1 = bf16[256,384]{1,0:T(8,128)(2,1)S(1)} custom-call(bf16[256,3072]{1,0:T(8,128)(2,1)} %lat_hbm.1, f32[3,1,3072]{2,1,0:T(1,128)} %bitcast.1, bf16[3,3072,384]{2,1,0:T(8,128)(2,1)} %wqkv_hbm.1, bf16[384,3072]{1,0:T(8,128)(2,1)} %wout_hbm.1, s32[32,32]{1,0:T(8,128)} %mask_ref.1, s32[32]{0:T(128)} %len_ref.1), custom_call_target="tpu_custom_call" | custom-call | tf_op jit(solution)/shard_map/attention_sublayer/pallas_call | solution.py:476
  63.5 0.7 %copy.8 = bf16[256,384]{1,0:T(8,128)(2,1)} copy(bf16[256,384]{1,0:T(8,128)(2,1)S(1)} %attention_sublayer.1) | data formatting | bytes 393216

commit v5 on v4

--- a/solution.py
+++ b/solution.py
@@ -9,7 +9,6 @@
 TOK = 256
 NZ, NY, NX = 8, 4, 4
 NEG = -1e30
-LOG2E = 1.4426950408889634
 HALF = TOK // 2
 PAUSE = 2500
 
@@ -130,69 +129,6 @@
     def q_remote(k):
         return remote(qsend.at[k], q.at[div(z, 2)], qs_sem.at[k], q_sem.at[div(z, 2)], at(z_=4 * c + k, c_=q_core))
 
-    def kv_local(k):
-        return (4 * c + k == z) & (slab_core == c)
-
-    def q_local(k):
-        return (4 * c + k == z) & (q_core == c)
-
-    def send_phase(phase, i):
-        k = nearest(i)
-        away = wrap(4 * c + k - z + NZ, NZ)
-        far = jnp.maximum(jnp.minimum(away, NZ - away), 1)
-
-        @pl.when((far == phase) & jnp.logical_not(kv_local(k)))
-        def _():
-            kv_remote(k).start()
-
-        @pl.when((jnp.maximum(far - 1, 1) == phase) & jnp.logical_not(q_local(k)))
-        def _():
-            q_remote(k).start()
-
-    def send_rest(phase):
-        @pl.loop(0, 3)
-        def _(i):
-            send_phase(phase, i)
-
-    @pl.loop(0, 3)
-    def _(i):
-        k = nearest(i)
-        with jax.named_scope("weights"):
-            for part in range(3):
-                weight_copy(k, part).wait()
-        made = jnp.dot(adapted[...], wqkv[k], preferred_element_type=jnp.float32)
-        kvsend[k] = made[:, 0:2 * HS].astype(jnp.bfloat16)
-        qsend[k] = (made[:, 2 * HS:3 * HS] * (LOG2E / HS**0.5)).astype(jnp.bfloat16)
-
-        @pl.when(kv_local(k))
-        def _():
-            kv[z, pl.ds(pl.multiple_of(y * TOK, TOK), TOK), :] = kvsend[k]
-
-        @pl.when(q_local(k))
-        def _():
-            q[div(z, 2)] = qsend[k]
-
-        send_phase(1, i)
-
-        @pl.when(i == 0)
-        def _():
-            for pair in others:
-                wout_send(*pair).start()
-
-    def order(t):
-        return wrap(z + jnp.where(rem(t, 2) == 1, NZ - div(t + 1, 2), div(t + 1, 2)), NZ)
-
-    def group_row(k):
-        return 2 * k + (1 - c if k % 2 else c)
-
-    def q_here(k):
-        return (group_row(k) == z) & (row_core == c)
-
-    def kv_wait(s, p, half=0, size=TOK):
-        start = half * HALF if size == HALF else 0
-        ref = piece(s, p, start, size)
-        remote(ref, ref, b_sem.at[0], kv_sem.at[s, p, half], at(c_=1 - c)).wait_recv()
-
     def hop(s, slot):
         p, device, half = (
             (y, at(y_=yp), None), (y, at(y_=ym), None), (y, at(c_=1 - c), None),
@@ -204,6 +140,74 @@
         ref = piece(s, p, start, size)
         return remote(ref, ref, b_sem.at[0], kv_sem.at[s, p, half or 0], device)
 
+    def kv_local(k):
+        return (4 * c + k == z) & (slab_core == c)
+
+    def q_local(k):
+        return (4 * c + k == z) & (q_core == c)
+
+    def send_phase(phase, i):
+        k = nearest(i)
+        away = wrap(4 * c + k - z + NZ, NZ)
+        far = jnp.maximum(jnp.minimum(away, NZ - away), 1)
+
+        @pl.when((far == phase) & jnp.logical_not(kv_local(k)))
+        def _():
+            kv_remote(k).start()
+
+        @pl.when((jnp.maximum(far - 1, 1) == phase) & jnp.logical_not(q_local(k)))
+        def _():
+            q_remote(k).start()
+
+    def send_rest(phase):
+        @pl.loop(0, 3)
+        def _(i):
+            send_phase(phase, i)
+
+    @pl.loop(0, 3)
+    def _(i):
+        k = nearest(i)
+        with jax.named_scope("weights"):
+            for part in range(3):
+                weight_copy(k, part).wait()
+        made = jnp.dot(adapted[...], wqkv[k], preferred_element_type=jnp.float32)
+        kvsend[k] = made[:, 0:2 * HS].astype(jnp.bfloat16)
+        qsend[k] = (made[:, 2 * HS:3 * HS] * (1.0 / HS**0.5)).astype(jnp.bfloat16)
+
+        @pl.when(kv_local(k))
+        def _():
+            kv[z, pl.ds(pl.multiple_of(y * TOK, TOK), TOK), :] = kvsend[k]
+
+        @pl.when(q_local(k))
+        def _():
+            q[div(z, 2)] = qsend[k]
+
+        @pl.when((i == 0) & kv_local(k))
+        def _():
+            for slot in range(3):
+                hop(z, slot).start()
+
+        send_phase(1, i)
+
+        @pl.when(i == 0)
+        def _():
+            for pair in others:
+                wout_send(*pair).start()
+
+    def order(t):
+        return wrap(z + jnp.where(rem(t, 2) == 1, NZ - div(t + 1, 2), div(t + 1, 2)), NZ)
+
+    def group_row(k):
+        return 2 * k + (1 - c if k % 2 else c)
+
+    def q_here(k):
+        return (group_row(k) == z) & (row_core == c)
+
+    def kv_wait(s, p, half=0, size=TOK):
+        start = half * HALF if size == HALF else 0
+        ref = piece(s, p, start, size)
+        remote(ref, ref, b_sem.at[0], kv_sem.at[s, p, half], at(c_=1 - c)).wait_recv()
+
     def relay(t, k, rows, mine):
         if k == 0:
             @pl.when((t < NZ) & mine[0])
@@ -215,8 +219,10 @@
                     with jax.named_scope("wait_z"):
                         kv_wait(s, y)
 
-                for slot in range(3):
-                    hop(s, slot).start()
+                @pl.when(jnp.logical_not((t == 0) & (row_core == c)))
+                def _():
+                    for slot in range(3):
+                        hop(s, slot).start()
 
             @pl.when((t >= 3) & jnp.logical_not(mine[3]))
             def _():
@@ -262,8 +268,8 @@
         ) + bias
         old = mx[k]
         new = jnp.maximum(old, jnp.max(score, axis=-1, keepdims=True))
-        keep = jnp.exp2(old - new)
-        weight = jnp.exp2(score - new[:, 0:1])
+        keep = jnp.exp(old - new)
+        weight = jnp.exp(score - new[:, 0:1])
         mx[k] = new
         total = weight[:, 0:HS]
         for i in range(1, NY * TOK // HS):
@@ -375,7 +381,7 @@
             (m, at(m_=xp), None), (m, at(m_=xm), None), (m, at(c_=1 - c), None),
             (xm, at(m_=xp), 0), (xm, at(c_=1 - c), None),
             (xp, at(m_=xm), 1), (xp, at(c_=1 - c), None),
-            (x2, at(c_=1 - c), None),
+            (x2, at(c_=1 - c), None), (m, at(m_=x2), None),
         )[slot]
         ref = att_piece(x, u, half)
         return remote(ref, ref, x_sem.at[0], att_sem.at[x, u, half or 0], device)
@@ -391,6 +397,10 @@
         def _():
             with jax.named_scope("wait_att"):
                 att_wait(m, 3 * c + k)
+
+        @pl.when(k == 2)
+        def _():
+            att_hop(k, 8).start()
 
         for slot in range(3):
             att_hop(k, slot).start()
@@ -405,12 +415,18 @@
     def _(k):
         with jax.named_scope("wait_xm"):
             att_wait(xm, 3 * c + k)
-        for slot in (3, 4):
-            att_hop(k, slot).start()
+        @pl.when(k < 2)
+        def _():
+            att_hop(k, 3).start()
+
+        att_hop(k, 4).start()
         with jax.named_scope("wait_xp"):
             att_wait(xp, 3 * c + k)
-        for slot in (5, 6):
-            att_hop(k, slot).start()
+        @pl.when(k < 2)
+        def _():
+            att_hop(k, 5).start()
+
+        att_hop(k, 6).start()
 
     def project_across(x):
         with jax.named_scope("wait_across"):
@@ -425,8 +441,15 @@
     @pl.loop(0, 3)
     def _(k):
         with jax.named_scope("wait_x2"):
-            att_wait(x2, 3 * c + k, 0)
-            att_wait(x2, 3 * c + k, 1)
+            @pl.when(k < 2)
+            def _():
+                att_wait(x2, 3 * c + k, 0)
+                att_wait(x2, 3 * c + k, 1)
+
+            @pl.when(k == 2)
+            def _():
+                att_wait(x2, 3 * c + k)
+
         att_hop(k, 7).start()
 
     project_across(xm)

time: 64.3 us -> 62.7 us (0.975)
  the two profiles are of different devices: /device:TPU:233 before, /device:TPU:1 now
where the time goes in v5:
time: 62.7 us; the launch traced here: 61.7 us
  Pallas kernels  61 us (97%)
  local copies, waits for them, and re-layouts  0.68 us (1%)
    pallas_call x1, Pallas kernels, shards(): pl.pallas_call(kernel, out_shape=pltpu.VMEM((tok, width), bf16), in_specs...  61 us

profile of v5, /device:TPU:1, one launch (start us, length us, event | category | flops | bytes accessed | tf_op | source)
XLA Modules:
  0.0 61.7 jit_solution(1420712461870354120)
XLA Ops:
  0.0 61.0 %attention_sublayer.1 = bf16[256,384]{1,0:T(8,128)(2,1)S(1)} custom-call(bf16[256,3072]{1,0:T(8,128)(2,1)} %lat_hbm.1, f32[3,1,3072]{2,1,0:T(1,128)} %bitcast.1, bf16[3,3072,384]{2,1,0:T(8,128)(2,1)} %wqkv_hbm.1, bf16[384,3072]{1,0:T(8,128)(2,1)} %wout_hbm.1, s32[32,32]{1,0:T(8,128)} %mask_ref.1, s32[32]{0:T(128)} %len_ref.1), custom_call_target="tpu_custom_call" | custom-call | tf_op jit(solution)/shard_map/attention_sublayer/pallas_call | solution.py:499
  61.0 0.7 %copy.8 = bf16[256,384]{1,0:T(8,128)(2,1)} copy(bf16[256,384]{1,0:T(8,128)(2,1)S(1)} %attention_sublayer.1) | data formatting | bytes 393216

commit v6 on v5

--- a/solution.py
+++ b/solution.py
@@ -78,7 +78,7 @@
     def weight_copy(k, part):
         cols = pl.ds(pl.multiple_of(k * HS, HS), HS)
         return pltpu.make_async_copy(
-            wqkv_hbm.at[(part + 1) % 3, :, cols], wqkv.at[k, :, pl.ds(part * HS, HS)], w_sem.at[k, part]
+            wqkv_hbm.at[(part + 1) % 3, :, cols], wqkv.at[k, :, pl.ds(part * HS, HS)], w_sem.at[k]
         )
 
     for i in range(3):
@@ -115,7 +115,7 @@
         cols = pl.ds(pl.multiple_of((2 * m_ + c_) * width, HS), width)
         return remote(
             wout_hbm.at[:, cols], wcol.at[m, own_rows, :],
-            wos_sem.at[0], wor_sem.at[dx, dc], at(m_=m_, c_=c_),
+            wos_sem.at[0], wor_sem.at[0], at(m_=m_, c_=c_),
         )
 
     others = [(dx, dc) for dx in range(NX) for dc in range(2) if (dx, dc) != (0, 0)]
@@ -168,8 +168,7 @@
     def _(i):
         k = nearest(i)
         with jax.named_scope("weights"):
-            for part in range(3):
-                weight_copy(k, part).wait()
+            pltpu.make_async_copy(wqkv.at[k], wqkv.at[k], w_sem.at[k]).wait()
         made = jnp.dot(adapted[...], wqkv[k], preferred_element_type=jnp.float32)
         kvsend[k] = made[:, 0:2 * HS].astype(jnp.bfloat16)
         qsend[k] = (made[:, 2 * HS:3 * HS] * (1.0 / HS**0.5)).astype(jnp.bfloat16)
@@ -407,8 +406,8 @@
 
     with jax.named_scope("wait_wout"):
         wout_copy.wait()
-        for pair in others:
-            wout_send(*pair).wait_recv()
+        seven = wqkv.at[0, pl.ds(0, 7 * width), pl.ds(0, width)]
+        remote(seven, seven, wos_sem.at[0], wor_sem.at[0], at(c_=1 - c)).wait_recv()
     branch[...] = project(m, c)
 
     @pl.loop(0, 3)
@@ -462,7 +461,7 @@
         out_ref[...] = (wide + mod[2, :, own_cols] * branch[...]).astype(jnp.bfloat16)
 
     def all_left(ref, sem):
-        remote(ref, ref, sem, wor_sem.at[0, 0], at(c_=1 - c)).wait_send()
+        remote(ref, ref, sem, wor_sem.at[0], at(c_=1 - c)).wait_send()
 
     with jax.named_scope("leave"):
         all_left(wqkv.at[0, pl.ds(0, 7 * width), pl.ds(0, width)], wos_sem.at[0])
@@ -508,8 +507,8 @@
             vmem((4, tok, HS), f32), vmem((4, tok, HS), f32), vmem((4, tok, HS), f32),
             vmem((4, tok, HS), bf16), vmem((NX, tok, 6 * HS), bf16), vmem((NX, 2 * width, width), bf16),
             vmem((tok, width), f32),
-            dma((3,)), dma((3, 3)), dma((3,)), dma((3,)), dma((NZ, NY, 2)), dma((4,)),
-            dma((1,)), dma((4,)), dma((NX, 6, 2)), dma((1,)), dma((1,)), dma((NX, 2)),
+            dma((3,)), dma((3,)), dma((3,)), dma((3,)), dma((NZ, NY, 2)), dma((4,)),
+            dma((1,)), dma((4,)), dma((NX, 6, 2)), dma((1,)), dma((1,)), dma((1,)),
         ],
         compiler_params=pltpu.CompilerParams(
             collective_id=0, has_side_effects=True, vmem_limit_bytes=60 * 1024 * 1024

time: 62.7 us -> 62.6 us (level)
  no operation moved by 1% of the time
where the time goes in v6:
time: 62.6 us; the launch traced here: 61.6 us
  Pallas kernels  60.9 us (97%)
  local copies, waits for them, and re-layouts  0.68 us (1%)
    pallas_call x1, Pallas kernels, shards(): pl.pallas_call(kernel, out_shape=pltpu.VMEM((tok, width), bf16), in_specs...  60.9 us

profile of v6, /device:TPU:1, one launch (start us, length us, event | category | flops | bytes accessed | tf_op | source)
XLA Modules:
  0.0 61.6 jit_solution(1606765398330882412)
XLA Ops:
  0.0 60.9 %attention_sublayer.1 = bf16[256,384]{1,0:T(8,128)(2,1)S(1)} custom-call(bf16[256,3072]{1,0:T(8,128)(2,1)} %lat_hbm.1, f32[3,1,3072]{2,1,0:T(1,128)} %bitcast.1, bf16[3,3072,384]{2,1,0:T(8,128)(2,1)} %wqkv_hbm.1, bf16[384,3072]{1,0:T(8,128)(2,1)} %wout_hbm.1, s32[32,32]{1,0:T(8,128)} %mask_ref.1, s32[32]{0:T(128)} %len_ref.1), custom_call_target="tpu_custom_call" | custom-call | tf_op jit(solution)/shard_map/attention_sublayer/pallas_call | solution.py:498
  60.9 0.7 %copy.8 = bf16[256,384]{1,0:T(8,128)(2,1)} copy(bf16[256,384]{1,0:T(8,128)(2,1)S(1)} %attention_sublayer.1) | data formatting | bytes 393216
